TPU v7x, 512 devices: a whole 4x4x16 slice. The times are simulated.
512 devices in a mesh: seq: 64 (over z, x_lo, core), tp: 8 (over x_hi, y).
Axes of the slice: x: 4 (x_hi: 2, x_lo: 2; x = x_hi * 2 + x_lo), y: 4, z: 16, core: 2. Of those that a mesh axis runs over, the one named last changes fastest.
Arguments:
- tokens: bfloat16 [32768, 3584], P(('seq', 'tp')), may hold values from -6 to 6
- pre_gain: float32 [3584], replicated, may hold values from 0.25 to 1.75
- post_gain: float32 [3584], replicated, may hold values from 0.25 to 1.75
- w_query: bfloat16 [3584, 4096], P('seq', 'tp'), may hold values from -0.09375 to 0.09375
- key_matrix: bfloat16 [3584, 2048], P('seq', 'tp'), may hold values from -0.09375 to 0.09375
- value_matrix: bfloat16 [3584, 2048], P('seq', 'tp'), may hold values from -0.09375 to 0.09375
- w_out: bfloat16 [4096, 3584], P('tp', 'seq'), may hold values from -0.09375 to 0.09375
Outputs:
- block_out: bfloat16 [32768, 3584], P(('seq', 'tp'))
All inputs are finite; a program needn't handle non-finite values.
Results may differ from a plain program's by a relative error of at most 0.014.
Values may be sent and summed in bfloat16 or wider, within the bound.
No kernel may reach another device: no remote copies, remote signals or barrier semaphores. Data moves between devices by JAX's collectives and lax.ppermute only.
A program may use at most 64 MiB of HBM per device.

v0:
```python
import jax
import jax.numpy as jnp
from jax import lax
from jax.sharding import Mesh
from jax.sharding import PartitionSpec as P

HEAD_SIZE = 256
BLOCK_TOKENS = 512
SEQ = ("seq_0", "seq_1", "seq_2")
TP = ("tp_0", "tp_1")
SEQ_TP = ("seq_0", "seq_1", "seq_2", "tp_0", "tp_1")


def to_every_tp(x):
    length = lax.axis_size(TP)
    return lax.all_to_all(jnp.broadcast_to(x[None], (length, *x.shape)), TP, 0, 0, tiled=True)


def weights_of_heads(slab):
    pair = ("seq_1", "seq_2")
    first = lax.ppermute(slab, pair, [(1, 0), (0, 2), (3, 1), (2, 3)])
    second = lax.ppermute(slab, pair, [(1, 2), (2, 1)])
    chip, core = (lax.axis_index("seq_1"), lax.axis_index("seq_2"))
    same = chip == core
    upper = jnp.where(same, jnp.where(core == 0, slab, first), jnp.where(core == 0, first, second))
    lower = jnp.where(same, jnp.where(core == 0, first, slab), jnp.where(core == 0, second, first))
    mine = jnp.concatenate([upper, lower], axis=0)
    return lax.all_gather(mine, ("seq_0", "seq_2"), axis=0, tiled=True)


def from_behind(x, axis, by):
    length = lax.axis_size(axis)
    pairs = [(i, i + by) for i in range(length) if 0 <= i + by < length]
    return lax.ppermute(x, axis, pairs)


def root_norm(values, gain):
    values = values.astype(jnp.float32)
    return values * lax.rsqrt(jnp.mean(values * values, axis=-1, keepdims=True) + 1e-06) * gain


def rotate_halves(values, token_positions):
    row_count = values.shape[0]
    shaped = values.reshape(row_count, -1, HEAD_SIZE)
    half_dim = HEAD_SIZE // 2
    freq = 10000.0 ** (-(jnp.arange(half_dim).astype(jnp.float32) * 2.0 / HEAD_SIZE))
    angle = token_positions[:, None] * freq[None, :]
    cosine = jnp.cos(angle)[:, None, :]
    sine_part = jnp.sin(angle)[:, None, :]
    first = shaped[..., :half_dim]
    second = shaped[..., half_dim:]
    turned = jnp.concatenate(
        [first * cosine - second * sine_part, second * cosine + first * sine_part], axis=-1
    )
    return turned.reshape(row_count, -1)


def attend(query_rows, keys_now, vals_now, keys_prior, vals_prior, offset_pos):
    length = query_rows.shape[0]
    kv_heads = keys_now.shape[1] // HEAD_SIZE
    repeat_heads = query_rows.shape[1] // (HEAD_SIZE * kv_heads)
    query_grouped = query_rows.reshape(length, kv_heads, repeat_heads, HEAD_SIZE)
    key_current = jnp.concatenate([keys_prior, keys_now], axis=0).reshape(
        2 * length, kv_heads, HEAD_SIZE
    )
    value_current = jnp.concatenate([vals_prior, vals_now], axis=0).reshape(
        2 * length, kv_heads, HEAD_SIZE
    )
    attention_scores = jnp.einsum(
        "cwap,bwp->wacb", query_grouped, key_current, preferred_element_type=jnp.float32
    )
    query_idx = jnp.arange(length)[:, None]
    key_idx = jnp.arange(2 * length)[None, :]
    key_pos = offset_pos - length + key_idx
    allowed = (key_idx > query_idx) & (key_idx <= query_idx + length) & (key_pos >= 0)
    weights = jnp.where(allowed, jnp.exp(attention_scores), 0.0)
    denominator = jnp.sum(weights, axis=-1)
    weight_narrow = weights.astype(jnp.bfloat16)
    reduced_output = jnp.einsum(
        "bpqu,ubm->qbpm", weight_narrow, value_current, preferred_element_type=jnp.float32
    )
    attended = reduced_output / jnp.transpose(denominator, (2, 0, 1))[..., None]
    return attended.astype(jnp.bfloat16).reshape(length, -1)


def local(tokens, pre_gain, post_gain, w_query, key_matrix, value_matrix, w_out):
    normalized_input = root_norm(tokens, pre_gain).astype(jnp.bfloat16)
    query_cols = w_query.shape[1]
    key_cols = key_matrix.shape[1]
    slab = jnp.concatenate([w_query, key_matrix, value_matrix, w_out.T], axis=1)
    gathered = weights_of_heads(slab)
    width = query_cols + 2 * key_cols
    piece = to_every_tp(normalized_input).reshape(-1, normalized_input.shape[1])
    joined = jnp.dot(piece, gathered[:, :width], preferred_element_type=jnp.float32)
    raw_q = joined[:, :query_cols]
    raw_k = joined[:, query_cols : query_cols + key_cols]
    raw_v = joined[:, query_cols + key_cols :]
    offset_pos = lax.axis_index(SEQ) * BLOCK_TOKENS
    token_positions = (offset_pos + jnp.arange(BLOCK_TOKENS)).astype(jnp.float32)
    query_rows = (rotate_halves(raw_q, token_positions) * HEAD_SIZE ** (-0.5)).astype(jnp.bfloat16)
    keys_now = rotate_halves(raw_k, token_positions).astype(jnp.bfloat16)
    vals_now = raw_v.astype(jnp.bfloat16)
    keys_prior, vals_prior = from_behind((keys_now, vals_now), SEQ, 1)
    attended = attend(query_rows, keys_now, vals_now, keys_prior, vals_prior, offset_pos)
    partial_value = lax.dot_general(
        attended, gathered[:, width:], (((1,), (1,)), ((), ())), preferred_element_type=jnp.float32
    )
    length = lax.axis_size(TP)
    pieces = partial_value.astype(jnp.bfloat16).reshape(length, -1, partial_value.shape[1])
    received = lax.all_to_all(pieces, TP, 0, 0, tiled=True)
    own_rows = jnp.sum(received.astype(jnp.float32), axis=0)
    mixed = root_norm(own_rows, post_gain)
    return (tokens.astype(jnp.float32) + mixed).astype(jnp.bfloat16)


def solution(mesh):
    finer = Mesh(mesh.devices.reshape(16, 2, 2, 2, 4), ("seq_0", "seq_1", "seq_2", "tp_0", "tp_1"))
    in_specs = (P(SEQ_TP, None), P(), P(), P(SEQ, TP), P(SEQ, TP), P(SEQ, TP), P(TP, SEQ))
    out_specs = P(SEQ_TP, None)
    return jax.shard_map(local, mesh=finer, in_specs=in_specs, out_specs=out_specs, check_vma=False)
```

profile of v0, /device:TPU:1, one launch (start us, length us, event | category | flops | bytes accessed | tf_op | source)
XLA Modules:
  0.0 190.8 jit_solution(14534941523644795251)
XLA Ops:
  6.5 0.9 pad_maximum_fusion.1
  7.4 8.7 %collective-permute-start = (bf16[56,1536]{1,0:T(8,128)(2,1)S(1)}, bf16[56,1536]{1,0:T(8,128)(2,1)S(1)}, u32[]{:S(2)}, u32[]{:S(2)}) collective-permute-start(bf16[56,1536]{1,0:T(8,128)(2,1)S(1)} %pad_maximum_fusion.1), channel_id=1, source_target_pairs={{8,0},{0,16},{24,8},{16,24},{9,1},{1,17},{25,9},{17,25},{10,2},{2,... | collective-permute-start | bytes 516104 | tf_op jit(solution)/shard_map/ppermute | solution.py:21
  16.2 1.9 %collective-permute-start.1 = (bf16[56,1536]{1,0:T(8,128)(2,1)S(1)}, bf16[56,1536]{1,0:T(8,128)(2,1)S(1)}, u32[]{:S(2)}, u32[]{:S(2)}) collective-permute-start(bf16[56,1536]{1,0:T(8,128)(2,1)S(1)} %pad_maximum_fusion.1), channel_id=1, source_target_pairs={{8,16},{16,8},{9,17},{17,9},{10,18},{18,10},{11,19},{19,11},{12,20... | collective-permute-start | bytes 516104 | tf_op jit(solution)/shard_map/ppermute | solution.py:22
  18.1 4.8 %collective-permute-done.1 = bf16[56,1536]{1,0:T(8,128)(2,1)S(1)} collective-permute-done((bf16[56,1536]{1,0:T(8,128)(2,1)S(1)}, bf16[56,1536]{1,0:T(8,128)(2,1)S(1)}, u32[]{:S(2)}, u32[]{:S(2)}) %collective-permute-start.1) | collective-permute-done | bytes 172064 | tf_op jit(solution)/shard_map/ppermute | solution.py:22
  22.9 1.0 select_select_fusion.1
  23.9 0.8 pad_maximum_fusion
  24.7 1.2 fusion.18
  25.9 1.2 fusion.20
  27.1 2.1 %broadcast_in_dim.8 = bf16[8,64,3584]{2,1,0:T(8,128)(2,1)} broadcast(bf16[64,3584]{1,0:T(8,128)(2,1)S(1)} %fusion.20), dimensions={1,2} | broadcast | bytes 4128768 | tf_op jit(solution)/shard_map/broadcast_in_dim | solution.py:16
  29.2 4.5 %all-to-all-start = ((bf16[8,64,3584]{2,1,0:T(8,128)(2,1)}), bf16[8,64,3584]{2,1,0:T(8,128)(2,1)}, u32[]{:S(2)}, u32[]{:S(2)}) async-start(bf16[8,64,3584]{2,1,0:T(8,128)(2,1)} %broadcast_in_dim.8), calls=%async_computation | async-start | bytes 7340032 | tf_op jit(solution)/shard_map/all_to_all | solution.py:16
  33.8 1.0 multiply_cosine_fusion
  35.2 38.8 %all-to-all-done = bf16[8,64,3584]{2,1,0:T(8,128)(2,1)} async-done(((bf16[8,64,3584]{2,1,0:T(8,128)(2,1)}), bf16[8,64,3584]{2,1,0:T(8,128)(2,1)}, u32[]{:S(2)}, u32[]{:S(2)}) %all-to-all-start) | async-done | bytes 3670048 | tf_op jit(solution)/shard_map/all_to_all | solution.py:16
  74.0 32.5 %all-gather.2.cloned.1.call-done = bf16[3584,1536]{1,0:T(8,128)(2,1)} async-done(((bf16[112,1536]{1,0:T(8,128)(2,1)}), bf16[3584,1536]{1,0:T(8,128)(2,1)}) %all-gather.2.cloned.1.call-update) | async-done | bytes 11010064 | tf_op jit(solution)/shard_map/all_gather | solution.py:28
  106.6 7.3 %fusion = f32[512,1024]{1,0:T(8,128)S(1)} fusion(bf16[512,3584]{1,0:T(8,128)(2,1)} %bitcast, bf16[3584,1536]{1,0:T(8,128)(2,1)} %all-gather.2.cloned.1.call-done), kind=kOutput, calls=%fused_computation | convolution fusion | flops 3758096384 | bytes 13107200 | tf_op jit(solution)/shard_map/dot_general | solution.py:94
  114.1 1.2 fusion.34
  115.3 0.7 maximum_bitcast_fusion.4
  116.0 3.2 %collective-permute-start.3 = (bf16[512,256]{1,0:T(8,128)(2,1)}, bf16[512,256]{1,0:T(8,128)(2,1)}, u32[]{:S(2)}, u32[]{:S(2)}) collective-permute-start(bf16[512,256]{1,0:T(8,128)(2,1)} %maximum_bitcast_fusion.4), channel_id=1, source_target_pairs={{0,8},{8,16},{16,24},{24,32},{32,40},{40,48},{48,56},{56,64},{64,7... | collective-permute-start | bytes 786440 | tf_op jit(solution)/shard_map/ppermute | solution.py:34
  120.3 2.1 %collective-permute-start.2 = (bf16[512,256]{1,0:T(8,128)(2,1)S(1)}, bf16[512,256]{1,0:T(8,128)(2,1)S(1)}, u32[]{:S(2)}, u32[]{:S(2)}) collective-permute-start(bf16[512,256]{1,0:T(8,128)(2,1)S(1)} %slice.56), channel_id=1, source_target_pairs={{0,8},{8,16},{16,24},{24,32},{32,40},{40,48},{48,56},{56,64},{64,7... | collective-permute-start | bytes 786440 | tf_op jit(solution)/shard_map/ppermute | solution.py:34
  122.9 2.1 %fusion.2 = (f32[2,512]{1,0:T(2,128)S(1)}, f32[1024,512,2]{1,0,2:T(8,128)S(1)}) fusion(pred[512,1024]{0,1:T(8,128)(4,1)S(1)} %fusion.10, f32[512,2,128]{2,0,1:T(8,128)S(1)} %get-tuple-element.6, f32[512,2,128]{2,0,1:T(8,128)S(1)} %get-tuple-element.5, bf16[512,256]{1,0:T(8,128)(2,1)} %maximum_bitcast_fusion.4, bf16[512,256]{1,0:T(8,128)(2,1)} %collective-permute-done.3), kind=kOutput, calls=%fused_computation.5 | convolution fusion | flops 540802048 | bytes 6295552 | tf_op jit(solution)/shard_map/cwap,bwp->wacb/dot_general | solution.py:69
  125.0 0.8 collective-permute-done.2
  125.8 1.0 divide_convert_fusion
  126.8 4.2 %convolution_convert_fusion = bf16[512,3584]{1,0:T(8,128)(2,1)S(1)} fusion(bf16[512,512]{0,1:T(8,128)(2,1)S(1)} %bitcast.54, bf16[3584,1536]{1,0:T(8,128)(2,1)} %all-gather.2.cloned.1.call-done), kind=kOutput, calls=%fused_computation.3 | convolution fusion | flops 1880883200 | bytes 7864320 | tf_op jit(solution)/shard_map/dot_general | solution.py:105
  131.0 51.1 %all_to_all.10 = bf16[8,64,3584]{2,1,0:T(8,128)(2,1)S(1)} all-to-all(bf16[8,64,3584]{2,1,0:T(8,128)(2,1)S(1)} %bitcast.51), channel_id=1, replica_groups=mesh['seq_0'=16,'seq_1'=2,'seq_2'=2,'tp_0'=2,'tp_1'=4] {'tp_0','tp_1'}, dimensions={0} | all-to-all | bytes 7340032 | tf_op jit(solution)/shard_map/all_to_all | solution.py:110
  183.0 1.0 fusion.21
  (23 shorter events, 3.1 us)
Async XLA Ops:
  6.5 100.0 %all-gather.2.cloned.1.call-start = ((), (), s32[]{:S(2)}) async-start(), calls=%async_computation.2 | async-start | bytes 11354112 | tf_op jit(solution)/shard_map/all_gather | solution.py:28
  7.4 10.7 %collective-permute-start = (bf16[56,1536]{1,0:T(8,128)(2,1)S(1)}, bf16[56,1536]{1,0:T(8,128)(2,1)S(1)}, u32[]{:S(2)}, u32[]{:S(2)}) collective-permute-start(bf16[56,1536]{1,0:T(8,128)(2,1)S(1)} %pad_maximum_fusion.1), channel_id=1, source_target_pairs={{8,0},{0,16},{24,8},{16,24},{9,1},{1,17},{25,9},{17,25},{10,2},{2,... | collective-permute-start | bytes 516104 | tf_op jit(solution)/shard_map/ppermute | solution.py:21
  16.2 6.7 %collective-permute-start.1 = (bf16[56,1536]{1,0:T(8,128)(2,1)S(1)}, bf16[56,1536]{1,0:T(8,128)(2,1)S(1)}, u32[]{:S(2)}, u32[]{:S(2)}) collective-permute-start(bf16[56,1536]{1,0:T(8,128)(2,1)S(1)} %pad_maximum_fusion.1), channel_id=1, source_target_pairs={{8,16},{16,8},{9,17},{17,9},{10,18},{18,10},{11,19},{19,11},{12,20... | collective-permute-start | bytes 516104 | tf_op jit(solution)/shard_map/ppermute | solution.py:22
  29.2 44.8 %all-to-all-start = ((bf16[8,64,3584]{2,1,0:T(8,128)(2,1)}), bf16[8,64,3584]{2,1,0:T(8,128)(2,1)}, u32[]{:S(2)}, u32[]{:S(2)}) async-start(bf16[8,64,3584]{2,1,0:T(8,128)(2,1)} %broadcast_in_dim.8), calls=%async_computation | async-start | bytes 7340032 | tf_op jit(solution)/shard_map/all_to_all | solution.py:16
  116.0 6.9 %collective-permute-start.3 = (bf16[512,256]{1,0:T(8,128)(2,1)}, bf16[512,256]{1,0:T(8,128)(2,1)}, u32[]{:S(2)}, u32[]{:S(2)}) collective-permute-start(bf16[512,256]{1,0:T(8,128)(2,1)} %maximum_bitcast_fusion.4), channel_id=1, source_target_pairs={{0,8},{8,16},{16,24},{24,32},{32,40},{40,48},{48,56},{56,64},{64,7... | collective-permute-start | bytes 786440 | tf_op jit(solution)/shard_map/ppermute | solution.py:34
  120.3 5.4 %collective-permute-start.2 = (bf16[512,256]{1,0:T(8,128)(2,1)S(1)}, bf16[512,256]{1,0:T(8,128)(2,1)S(1)}, u32[]{:S(2)}, u32[]{:S(2)}) collective-permute-start(bf16[512,256]{1,0:T(8,128)(2,1)S(1)} %slice.56), channel_id=1, source_target_pairs={{0,8},{8,16},{16,24},{24,32},{32,40},{40,48},{48,56},{56,64},{64,7... | collective-permute-start | bytes 786440 | tf_op jit(solution)/shard_map/ppermute | solution.py:34
  182.0 1.0 copy-start
  182.0 1.0 copy-start.1
Sparse Core Ops, SparseCore 0:
  24.8 81.6 all-gather.1
where the time goes:
time: 191 us
  waiting for transfers between devices  77.1 us (40%)
  blocking collectives  51.1 us (27%)
  starting transfers between devices  20.6 us (11%)
  matrix products  14.6 us (8%)
  between operations  13.6 us (7%)
  other arithmetic  10.2 us (5%)
  local copies, waits for them, and re-layouts  3.64 us (2%)
    all_to_all x1, blocking collectives, local(): received = lax.all_to_all(pieces, TP, 0, 0, tiled=True)  51.1 us
    all_to_all x1, waiting for transfers between devices, to_every_tp(): lax.all_to_all(jnp.broadcast_to(x[None], (length, *x.shape)), TP, 0, 0, t...  38.8 us
    all_gather x1, waiting for transfers between devices, weights_of_heads(): return lax.all_gather(mine, ('seq_0', 'seq_2'), axis=0, tiled=True)  32.5 us
    ppermute x1, starting transfers between devices, weights_of_heads(): first = lax.ppermute(slab, pair, [(1, 0), (0, 2), (3, 1), (2, 3)])  8.75 us
    dot_general x1, matrix products, local(): jnp.dot(piece, gathered[:, :width], preferred_element_type=jnp.float32)  7.31 us
    ppermute x2, starting transfers between devices, from_behind(): return lax.ppermute(x, axis, pairs)  5.39 us
    ppermute x1, waiting for transfers between devices, weights_of_heads(): second = lax.ppermute(slab, pair, [(1, 2), (2, 1)])  4.78 us
    all_to_all x1, starting transfers between devices, to_every_tp(): lax.all_to_all(jnp.broadcast_to(x[None], (length, *x.shape)), TP, 0, 0, t...  4.5 us
  transfers between devices with their start and end apart: 6, of which 5 were waited for; matrix products, arithmetic and copies ran while one was open for 5% of the time, Pallas kernels for 0%

commit v1 on v0

--- a/solution.py
+++ b/solution.py
@@ -25,7 +25,12 @@
     upper = jnp.where(same, jnp.where(core == 0, slab, first), jnp.where(core == 0, first, second))
     lower = jnp.where(same, jnp.where(core == 0, first, slab), jnp.where(core == 0, second, first))
     mine = jnp.concatenate([upper, lower], axis=0)
-    return lax.all_gather(mine, ("seq_0", "seq_2"), axis=0, tiled=True)
+    return jnp.concatenate(
+        lax.all_to_all(
+            jnp.stack([mine] * lax.axis_size(("seq_0", "seq_2"))), ("seq_0", "seq_2"), 0, 0
+        ),
+        axis=0,
+    )
 
 
 def from_behind(x, axis, by):

time: 191 us -> 637 us (3.34); the launches traced: 191 us -> 630 us
  waiting for transfers between devices: 77.1 us -> 511 us
  starting transfers between devices: 20.6 us -> 36.3 us
  between operations: 13.6 us -> 0.27 us
    all_to_all x0 -> x1, waiting for transfers between devices: none -> 472 us  [weights_of_heads(): lax.all_to_all(jnp.stack([mine] * lax.axis_size(('seq_0', 'seq_2'))), ('s...]
    all_to_all x1, waiting for transfers between devices: 38.8 us -> 0.01 us  [to_every_tp(): lax.all_to_all(jnp.broadcast_to(x[None], (length, *x.shape)), TP, 0, 0, t...]
    ppermute x1, waiting for transfers between devices: 0.01 us -> 36 us  [weights_of_heads(): first = lax.ppermute(slab, pair, [(1, 0), (0, 2), (3, 1), (2, 3)])]
    all_gather x1 -> x0, waiting for transfers between devices: 32.5 us -> none  [weights_of_heads(): return lax.all_gather(mine, ('seq_0', 'seq_2'), axis=0, tiled=True)]
    all_to_all x0 -> x1, starting transfers between devices: none -> 15.9 us  [weights_of_heads(): lax.all_to_all(jnp.stack([mine] * lax.axis_size(('seq_0', 'seq_2'))), ('s...]
  transfers between devices with their start and end apart: 6 -> 6, of which waited for: 5 -> 5; matrix products, arithmetic and copies ran while one was open for 5% -> 1% of each run, Pallas kernels for 0% -> 0%
where the time goes in v1:
time: 637 us; the launch traced here: 630 us
  waiting for transfers between devices  511 us (80%)
  blocking collectives  51.4 us (8%)
  starting transfers between devices  36.3 us (6%)
  matrix products  14.6 us (2%)
  local copies, waits for them, and re-layouts  8.91 us (1%)
  other arithmetic  7.7 us (1%)
    all_to_all x1, waiting for transfers between devices, weights_of_heads(): lax.all_to_all(jnp.stack([mine] * lax.axis_size(('seq_0', 'seq_2'))), ('s...  472 us
    all_to_all x1, blocking collectives, local(): received = lax.all_to_all(pieces, TP, 0, 0, tiled=True)  51.4 us
    ppermute x1, waiting for transfers between devices, weights_of_heads(): first = lax.ppermute(slab, pair, [(1, 0), (0, 2), (3, 1), (2, 3)])  36 us
    all_to_all x1, starting transfers between devices, weights_of_heads(): lax.all_to_all(jnp.stack([mine] * lax.axis_size(('seq_0', 'seq_2'))), ('s...  15.9 us
  transfers between devices with their start and end apart: 6, of which 5 were waited for; matrix products, arithmetic and copies ran while one was open for 1% of the time, Pallas kernels for 0%

profile of v1, /device:TPU:1, one launch (start us, length us, event | category | flops | bytes accessed | tf_op | source)
XLA Modules:
  0.0 629.8 jit_solution(6682666687921325486)
XLA Ops:
  0.0 1.2 fusion.18
  1.2 1.2 fusion.20
  2.4 2.1 broadcast_in_dim.8
  4.5 7.6 %all-to-all-start = ((bf16[8,64,3584]{2,1,0:T(8,128)(2,1)}), bf16[8,64,3584]{2,1,0:T(8,128)(2,1)}, u32[]{:S(2)}, u32[]{:S(2)}) async-start(bf16[8,64,3584]{2,1,0:T(8,128)(2,1)} %broadcast_in_dim.8), calls=%async_computation | async-start | bytes 7340032 | tf_op jit(solution)/shard_map/all_to_all | solution.py:16
  12.2 5.8 collective-permute-start
  18.0 1.9 collective-permute-start.1
  20.0 36.0 %collective-permute-done = bf16[56,1536]{1,0:T(8,128)(2,1)S(1)} collective-permute-done((bf16[56,1536]{1,0:T(8,128)(2,1)S(1)}, bf16[56,1536]{1,0:T(8,128)(2,1)S(1)}, u32[]{:S(2)}, u32[]{:S(2)}) %collective-permute-start) | collective-permute-done | bytes 172064 | tf_op jit(solution)/shard_map/ppermute | solution.py:21
  55.9 1.1 collective-permute-done.1
  57.2 5.3 stack.2
  62.5 15.9 %all-to-all-start.1 = ((bf16[32,112,1536]{2,1,0:T(8,128)(2,1)}), bf16[32,112,1536]{2,1,0:T(8,128)(2,1)}, u32[]{:S(2)}, u32[]{:S(2)}) async-start(bf16[32,112,1536]{2,1,0:T(8,128)(2,1)} %stack.2), calls=%async_computation.1 | async-start | bytes 22020096 | tf_op jit(solution)/shard_map/all_to_all | solution.py:29
  78.5 1.0 multiply_cosine_fusion
  79.9 472.4 %all-to-all-done.1 = bf16[32,112,1536]{2,1,0:T(8,128)(2,1)} async-done(((bf16[32,112,1536]{2,1,0:T(8,128)(2,1)}), bf16[32,112,1536]{2,1,0:T(8,128)(2,1)}, u32[]{:S(2)}, u32[]{:S(2)}) %all-to-all-start.1) | async-done | bytes 11010080 | tf_op jit(solution)/shard_map/all_to_all | solution.py:29
  552.3 7.3 %fusion = f32[512,1024]{1,0:T(8,128)S(1)} fusion(bf16[512,3584]{1,0:T(8,128)(2,1)} %bitcast, bf16[3584,1536]{1,0:T(8,128)(2,1)} %bitcast.2), kind=kOutput, calls=%fused_computation | convolution fusion | flops 3758096384 | bytes 13107200 | tf_op jit(solution)/shard_map/dot_general | solution.py:99
  559.8 1.2 fusion.34
  561.0 0.7 maximum_bitcast_fusion.4
  561.8 3.1 collective-permute-start.3
  564.9 0.7 reshape.181
  565.9 1.9 collective-permute-start.2
  568.5 2.1 fusion.2
  570.6 0.6 collective-permute-done.2
  571.2 1.0 divide_convert_fusion
  572.2 4.2 convolution_convert_fusion
  576.4 51.4 %all_to_all.15 = bf16[8,64,3584]{2,1,0:T(8,128)(2,1)S(1)} all-to-all(bf16[8,64,3584]{2,1,0:T(8,128)(2,1)S(1)} %bitcast.52), channel_id=1, replica_groups=mesh['seq_0'=16,'seq_1'=2,'seq_2'=2,'tp_0'=2,'tp_1'=4] {'tp_0','tp_1'}, dimensions={0} | all-to-all | bytes 7340032 | tf_op jit(solution)/shard_map/all_to_all | solution.py:115
  628.8 1.0 fusion.21
  (31 shorter events, 2.8 us)
Async XLA Ops:
  4.5 7.6 %copy-start.1 = (bf16[512,56]{0,1:T(8,128)(2,1)S(1)}, bf16[512,56]{0,1:T(8,128)(2,1)}, u32[]{:S(2)}) copy-start(bf16[512,56]{0,1:T(8,128)(2,1)} %param.13) | copy-start | bytes 172036
  4.5 7.6 %copy-start.2 = (bf16[56,512]{1,0:T(8,128)(2,1)S(1)}, bf16[56,512]{1,0:T(8,128)(2,1)}, u32[]{:S(2)}) copy-start(bf16[56,512]{1,0:T(8,128)(2,1)} %param.10) | copy-start | bytes 172036
  4.5 7.6 %copy-start.3 = (bf16[56,256]{1,0:T(8,128)(2,1)S(1)}, bf16[56,256]{1,0:T(8,128)(2,1)}, u32[]{:S(2)}) copy-start(bf16[56,256]{1,0:T(8,128)(2,1)} %param.12) | copy-start | bytes 86020
  4.5 7.6 %copy-start.4 = (bf16[56,256]{1,0:T(8,128)(2,1)S(1)}, bf16[56,256]{1,0:T(8,128)(2,1)}, u32[]{:S(2)}) copy-start(bf16[56,256]{1,0:T(8,128)(2,1)} %param.11) | copy-start | bytes 86020
  4.5 52.7 %all-to-all-start = ((bf16[8,64,3584]{2,1,0:T(8,128)(2,1)}), bf16[8,64,3584]{2,1,0:T(8,128)(2,1)}, u32[]{:S(2)}, u32[]{:S(2)}) async-start(bf16[8,64,3584]{2,1,0:T(8,128)(2,1)} %broadcast_in_dim.8), calls=%async_computation | async-start | bytes 7340032 | tf_op jit(solution)/shard_map/all_to_all | solution.py:16
  12.2 43.7 %collective-permute-start = (bf16[56,1536]{1,0:T(8,128)(2,1)S(1)}, bf16[56,1536]{1,0:T(8,128)(2,1)S(1)}, u32[]{:S(2)}, u32[]{:S(2)}) collective-permute-start(bf16[56,1536]{1,0:T(8,128)(2,1)S(1)} %pad_maximum_fusion.1), channel_id=1, source_target_pairs={{8,0},{0,16},{24,8},{16,24},{9,1},{1,17},{25,9},{17,25},{10,2},{2,... | collective-permute-start | bytes 516104 | tf_op jit(solution)/shard_map/ppermute | solution.py:21
  18.0 39.0 %collective-permute-start.1 = (bf16[56,1536]{1,0:T(8,128)(2,1)S(1)}, bf16[56,1536]{1,0:T(8,128)(2,1)S(1)}, u32[]{:S(2)}, u32[]{:S(2)}) collective-permute-start(bf16[56,1536]{1,0:T(8,128)(2,1)S(1)} %pad_maximum_fusion.1), channel_id=1, source_target_pairs={{8,16},{16,8},{9,17},{17,9},{10,18},{18,10},{11,19},{19,11},{12,20... | collective-permute-start | bytes 516104 | tf_op jit(solution)/shard_map/ppermute | solution.py:22
  62.5 489.8 %all-to-all-start.1 = ((bf16[32,112,1536]{2,1,0:T(8,128)(2,1)}), bf16[32,112,1536]{2,1,0:T(8,128)(2,1)}, u32[]{:S(2)}, u32[]{:S(2)}) async-start(bf16[32,112,1536]{2,1,0:T(8,128)(2,1)} %stack.2), calls=%async_computation.1 | async-start | bytes 22020096 | tf_op jit(solution)/shard_map/all_to_all | solution.py:29
  561.8 6.7 %collective-permute-start.3 = (bf16[512,256]{1,0:T(8,128)(2,1)}, bf16[512,256]{1,0:T(8,128)(2,1)}, u32[]{:S(2)}, u32[]{:S(2)}) collective-permute-start(bf16[512,256]{1,0:T(8,128)(2,1)} %maximum_bitcast_fusion.4), channel_id=1, source_target_pairs={{0,8},{8,16},{16,24},{24,32},{32,40},{40,48},{48,56},{56,64},{64,7... | collective-permute-start | bytes 786440 | tf_op jit(solution)/shard_map/ppermute | solution.py:39
  565.9 5.3 collective-permute-start.2
  627.8 1.0 copy-start
  627.8 1.0 copy-start.5
